TPU v7x, 32 devices: a whole 2x2x4 slice. The times are simulated.
32 devices in a mesh: vocab: 8 (over z, x), seq: 4 (over y, core).
Axes of the slice: x: 2, y: 2, z: 4, core: 2. Of those that a mesh axis runs over, the one named last changes fastest.
Arguments:
- hidden: bfloat16 [1536, 7168], P(('vocab', 'seq')), may hold values from -64 to 64
- head_matrix: bfloat16 [7168, 8192], P('seq', 'vocab'), may hold values from -4 to 4
- targets: int32 [1536], P(('vocab', 'seq')), may hold values from 0 to 8191
Outputs:
- logprob: float32 [1536], P(('vocab', 'seq'))
All inputs are finite; a program needn't handle non-finite values.
Results may differ from a plain program's by a relative error of at most 0.0003.
Values may be sent and summed in bfloat16 or wider, within the bound.
A program may use at most 128 MiB of HBM per device.

v0:
```python
import jax
import jax.numpy as jnp
from jax import lax
from jax.sharding import PartitionSpec as P


def row_stats(logits, wanted, offset):
    maximum = jnp.max(logits, axis=1)
    expsum = jnp.sum(jnp.exp(logits - maximum[:, None]), axis=1)
    columns = lax.broadcasted_iota(jnp.int32, logits.shape, 1) + offset
    picked = jnp.sum(jnp.where(columns == wanted[:, None], logits, 0.0), axis=1)
    return (maximum, expsum, picked)


def local(hidden, head_matrix, targets):
    vocab_count = lax.axis_size("vocab")
    columns_dev = head_matrix.shape[1]
    tokens_dev = hidden.shape[0]
    offset = lax.axis_index("vocab") * columns_dev
    full_head = lax.all_gather(head_matrix, "seq", axis=0, tiled=True)
    logits = jnp.dot(
        lax.all_gather(hidden, "vocab", axis=0, tiled=True),
        full_head,
        preferred_element_type=jnp.float32,
    )
    row_values = row_stats(logits, lax.all_gather(targets, "vocab", axis=0, tiled=True), offset)
    maximum, expsum, picked = tuple((part_stat for part_stat in row_values))
    shaped = tuple(
        (values.reshape(vocab_count, tokens_dev) for values in (maximum, expsum, picked))
    )
    maxima, expsums, pickeds = lax.all_to_all(
        shaped, "vocab", split_axis=0, concat_axis=0, tiled=True
    )
    maximum = jnp.max(maxima, axis=0)
    expsum = jnp.sum(expsums * jnp.exp(maxima - maximum[None, :]), axis=0)
    picked = jnp.sum(pickeds, axis=0)
    return picked - (maximum + jnp.log(expsum))


def solution(mesh):
    return jax.shard_map(
        local,
        mesh=mesh,
        in_specs=(P(("vocab", "seq"), None), P("seq", "vocab"), P(("vocab", "seq"))),
        out_specs=P(("vocab", "seq")),
        check_vma=False,
    )
```

profile of v0, /device:TPU:0, one launch (start us, length us, event | category | flops | bytes accessed | tf_op | source)
XLA Modules:
  0.0 245.6 jit_solution(12284226454279272466)
XLA Ops:
  6.5 0.0 all-gather.3.cloned.1.call-start
  6.5 0.7 all-gather.3.cloned.1.call-update
  7.3 0.0 copy-start.1
  7.3 0.0 copy-start
  7.3 0.0 all-gather.5.cloned.1.call-start
  7.3 0.7 all-gather.5.cloned.1.call-update
  8.0 0.0 copy-done.1
  8.0 0.6 dynamic-slice
  9.3 0.0 copy-done
  9.3 0.2 dynamic-update-slice
  9.5 13.1 %all-reduce = s32[384]{0:T(512)S(1)} all-reduce(s32[384]{0:T(512)S(1)} %dynamic-update-slice), channel_id=1, replica_groups=mesh['vocab'=8,'seq'=4] {'vocab'}, use_global_device_ids=true, to_apply=%add | all-reduce | flops 384 | bytes 3072
  22.6 78.7 %all-gather.3.cloned.1.call-done = bf16[384,7168]{1,0:T(8,128)(2,1)} async-done(((bf16[48,7168]{1,0:T(8,128)(2,1)}), bf16[384,7168]{1,0:T(8,128)(2,1)}) %all-gather.3.cloned.1.call-update) | async-done | bytes 5505040 | tf_op jit(solution)/shard_map/all_gather | solution.py:22
  101.4 93.7 %all-gather.5.cloned.1.call-done = bf16[7168,1024]{1,0:T(8,128)(2,1)} async-done(((bf16[1792,1024]{1,0:T(8,128)(2,1)}), bf16[7168,1024]{1,0:T(8,128)(2,1)}) %all-gather.5.cloned.1.call-update) | async-done | bytes 14680080 | tf_op jit(solution)/shard_map/all_gather | solution.py:20
  195.1 11.0 %fusion = (f32[384]{0:T(512)S(1)}, f32[384,1024]{1,0:T(8,128)S(1)}) fusion(bf16[384,7168]{1,0:T(8,128)(2,1)} %all-gather.3.cloned.1.call-done, bf16[7168,1024]{1,0:T(8,128)(2,1)} %all-gather.5.cloned.1.call-done), kind=kOutput, calls=%fused_computation.5 | convolution fusion | flops 5637537280 | bytes 21759488 | tf_op jit(solution)/shard_map/dot_general | solution.py:21
  206.1 0.7 all_to_all.24
  206.7 5.5 %all-to-all-start.1 = ((f32[8,1,48]{2,1,0:T(1,128)}), f32[8,1,48]{2,1,0:T(1,128)S(1)}, u32[]{:S(2)}, u32[]{:S(2)}) async-start(f32[8,1,48]{2,1,0:T(1,128)} %all_to_all.24), calls=%async_computation.1 | async-start | bytes 8192 | tf_op jit(solution)/shard_map/all_to_all | solution.py:31
  212.3 0.5 exponential_reduce_fusion
  212.8 0.7 all_to_all.22
  213.4 5.3 %all-to-all-done.1 = f32[8,1,48]{2,1,0:T(1,128)S(1)} async-done(((f32[8,1,48]{2,1,0:T(1,128)}), f32[8,1,48]{2,1,0:T(1,128)S(1)}, u32[]{:S(2)}, u32[]{:S(2)}) %all-to-all-start.1) | async-done | bytes 1568 | tf_op jit(solution)/shard_map/all_to_all | solution.py:31
  218.7 3.3 %all-to-all-start = ((f32[8,1,48]{2,1,0:T(1,128)}), f32[8,1,48]{2,1,0:T(1,128)S(1)}, u32[]{:S(2)}, u32[]{:S(2)}) async-start(f32[8,1,48]{2,1,0:T(1,128)} %all_to_all.22), calls=%async_computation | async-start | bytes 8192 | tf_op jit(solution)/shard_map/all_to_all | solution.py:31
  222.1 0.7 all_to_all.26
  222.8 5.8 %all-to-all-done = f32[8,1,48]{2,1,0:T(1,128)S(1)} async-done(((f32[8,1,48]{2,1,0:T(1,128)}), f32[8,1,48]{2,1,0:T(1,128)S(1)}, u32[]{:S(2)}, u32[]{:S(2)}) %all-to-all-start) | async-done | bytes 1568 | tf_op jit(solution)/shard_map/all_to_all | solution.py:31
  228.5 3.2 %all-to-all-start.2 = ((f32[8,1,48]{2,1,0:T(1,128)}), f32[8,1,48]{2,1,0:T(1,128)S(1)}, u32[]{:S(2)}, u32[]{:S(2)}) async-start(f32[8,1,48]{2,1,0:T(1,128)} %all_to_all.26), calls=%async_computation.2 | async-start | bytes 8192 | tf_op jit(solution)/shard_map/all_to_all | solution.py:31
  231.8 6.4 %all-to-all-done.2 = f32[8,1,48]{2,1,0:T(1,128)S(1)} async-done(((f32[8,1,48]{2,1,0:T(1,128)}), f32[8,1,48]{2,1,0:T(1,128)S(1)}, u32[]{:S(2)}, u32[]{:S(2)}) %all-to-all-start.2) | async-done | bytes 1568 | tf_op jit(solution)/shard_map/all_to_all | solution.py:31
  238.2 0.5 add_subtract_fusion
  (5 shorter events, 0.1 us)
Async XLA Ops:
  6.5 94.9 %all-gather.3.cloned.1.call-start = ((), (), s32[]{:S(2)}) async-start(), calls=%async_computation.3 | async-start | bytes 6193152 | tf_op jit(solution)/shard_map/all_gather | solution.py:22
  7.3 0.8 copy-start.1
  7.3 2.0 copy-start
  7.3 187.8 %all-gather.5.cloned.1.call-start = ((), (), s32[]{:S(2)}) async-start(), calls=%async_computation.4 | async-start | bytes 18350080 | tf_op jit(solution)/shard_map/all_gather | solution.py:20
  206.7 12.0 %all-to-all-start.1 = ((f32[8,1,48]{2,1,0:T(1,128)}), f32[8,1,48]{2,1,0:T(1,128)S(1)}, u32[]{:S(2)}, u32[]{:S(2)}) async-start(f32[8,1,48]{2,1,0:T(1,128)} %all_to_all.24), calls=%async_computation.1 | async-start | bytes 8192 | tf_op jit(solution)/shard_map/all_to_all | solution.py:31
  218.7 9.8 %all-to-all-start = ((f32[8,1,48]{2,1,0:T(1,128)}), f32[8,1,48]{2,1,0:T(1,128)S(1)}, u32[]{:S(2)}, u32[]{:S(2)}) async-start(f32[8,1,48]{2,1,0:T(1,128)} %all_to_all.22), calls=%async_computation | async-start | bytes 8192 | tf_op jit(solution)/shard_map/all_to_all | solution.py:31
  228.5 9.7 %all-to-all-start.2 = ((f32[8,1,48]{2,1,0:T(1,128)}), f32[8,1,48]{2,1,0:T(1,128)S(1)}, u32[]{:S(2)}, u32[]{:S(2)}) async-start(f32[8,1,48]{2,1,0:T(1,128)} %all_to_all.26), calls=%async_computation.2 | async-start | bytes 8192 | tf_op jit(solution)/shard_map/all_to_all | solution.py:31
Sparse Core Ops, SparseCore 0:
  9.5 91.8 all-gather.2
  102.9 92.1 all-gather.4
where the time goes:
time: 246 us
  waiting for transfers between devices  191 us (78%)
  between operations  14.1 us (6%)
  blocking collectives  13.1 us (5%)
  starting transfers between devices  12.1 us (5%)
  matrix products  11 us (4%)
  local copies, waits for them, and re-layouts  2.88 us (1%)
    all_gather x1, waiting for transfers between devices, local(): full_head = lax.all_gather(head_matrix, 'seq', axis=0, tiled=True)  93.7 us
    all_gather x1, waiting for transfers between devices, local(): lax.all_gather(hidden, 'vocab', axis=0, tiled=True)  78.7 us
    all_to_all x3, waiting for transfers between devices, local(): lax.all_to_all(shaped, 'vocab', split_axis=0, concat_axis=0, tiled=True)  17.4 us
    unnamed x1, blocking collectives  13.1 us
    all_to_all x3, starting transfers between devices, local(): lax.all_to_all(shaped, 'vocab', split_axis=0, concat_axis=0, tiled=True)  12.1 us
    dot_general x1, matrix products, local(): jnp.dot(lax.all_gather(hidden, 'vocab', axis=0, tiled=True), full_head, p...  11 us
  transfers between devices with their start and end apart: 5, of which 5 were waited for; matrix products, arithmetic and copies ran while one was open for 1% of the time, Pallas kernels for 0%

commit v1 on v0

v1 whole, which is shorter than its diff:
```python
import functools

import jax
import jax.numpy as jnp
from jax import lax
from jax.experimental import pallas as pl
from jax.experimental.pallas import tpu as pltpu
from jax.sharding import PartitionSpec as P

MESH = pl.DeviceIdType.MESH
TILE = 256


def ring_index(position, n):
    half = n // 2
    p = lax.rem(position + 2 * n, n)
    low = p // half
    high = jnp.where(low == 0, p, n - 1 - p)
    return high * 2 + low


def kernel(
    n, hidden, head, targets, out,
    x, w, wanted, part, other, stats, gathered,
    local_sem, swap_tx, swap_rx, ring_tx, ring_rx, part_tx, part_rx, stat_tx, stat_rx,
):
    half = n // 2
    width = head.shape[0]
    columns = head.shape[1]
    rows = hidden.shape[0]
    tile = min(TILE, columns)
    v = lax.axis_index("vocab")
    s = lax.axis_index("seq")
    y, c = s // 2, lax.rem(s, 2)
    low, high = lax.rem(v, 2), v // 2
    position = jnp.where(low == 0, high, n - 1 - high)
    ring = ((ring_index(position + 1, n), s), (ring_index(position - 1, n), s))
    y_mate = (v, (1 - y) * 2 + c)
    c_mate = (v, y * 2 + 1 - c)

    barrier = pltpu.get_barrier_semaphore()
    for device in (*ring, y_mate, c_mate):
        pl.semaphore_signal(barrier, inc=1, device_id=device, device_id_type=MESH)
    pl.semaphore_wait(barrier, 4)

    def remote(src, dst, tx, rx, device):
        return pltpu.make_async_remote_copy(
            src_ref=src, dst_ref=dst, send_sem=tx, recv_sem=rx, device_id=device, device_id_type=MESH
        )

    def block_at(direction, d):
        return ring_index(position - d if direction == 0 else position + d, n)

    def chunk_ref(block, ch):
        if ch == 4:
            return wanted.at[block]
        unit = y if ch < 2 else 1 - y
        return x.at[block, ch % 2, unit]

    def hop(direction, d, ch, src=None):
        dst = chunk_ref(block_at(direction, d), ch)
        return remote(
            dst if src is None else src, dst,
            ring_tx.at[direction, d, ch], ring_rx.at[direction, d + 1, ch], ring[direction],
        )

    def arrived(direction, d, ch):
        dst = chunk_ref(block_at(direction, d), ch)
        remote(dst, dst, ring_tx.at[direction, d - 1, ch], ring_rx.at[direction, d, ch], ring[direction]).wait_recv()

    def hidden_piece(half_y, h):
        start = pl.multiple_of((half_y * 2 + h) * width, width)
        return hidden.at[:, pl.ds(start, width)]

    own = []
    for h in range(2):
        for direction in range(2):
            hop(direction, 0, h, hidden_piece(y, h)).start()
    swaps = [
        remote(hidden_piece(1 - y, h), x.at[v, h, y], swap_tx.at[h], swap_rx.at[h], y_mate) for h in range(2)
    ]
    for swap in swaps:
        swap.start()
    for direction in range(2):
        hop(direction, 0, 4, targets).start()
    head_swap = remote(head, w.at[c], swap_tx.at[2], swap_rx.at[2], c_mate)
    head_swap.start()
    own.append(pltpu.make_async_copy(head, w.at[c], local_sem.at[0]))
    own.append(pltpu.make_async_copy(targets, wanted.at[v], local_sem.at[1]))
    for h in range(2):
        own.append(pltpu.make_async_copy(hidden_piece(y, h), x.at[v, h, y], local_sem.at[2 + h]))
    for copy in own:
        copy.start()

    def multiply(block):
        @pl.loop(0, columns // tile)
        def _(j):
            at = pl.ds(pl.multiple_of(j * tile, tile), tile)
            total = None
            for h in range(2):
                term = jnp.dot(
                    x[block, h].reshape(2 * rows, width), w[h, :, at], preferred_element_type=jnp.float32
                )
                total = term if total is None else total + term
            part[block, :, :, at] = total.reshape(2, rows, tile)

    def multiply_unit(block, unit):
        @pl.loop(0, columns // tile)
        def _(j):
            at = pl.ds(pl.multiple_of(j * tile, tile), tile)
            total = None
            for h in range(2):
                term = jnp.dot(x[block, h, unit], w[h, :, at], preferred_element_type=jnp.float32)
                total = term if total is None else total + term
            part[block, unit, :, at] = total

    def part_copy(block):
        return remote(part.at[block, 1 - y], other.at[block], part_tx.at[block], part_rx.at[block], y_mate)

    def stat_copy(block):
        return remote(stats.at[block], gathered.at[v], stat_tx.at[block], stat_rx.at[v], (block, s))

    def row_stats(block):
        part_copy(block).wait_recv()
        logits = part[block, y] + other[block]
        maximum = jnp.max(logits, axis=1, keepdims=True)
        expsum = jnp.sum(jnp.exp(logits - maximum), axis=1, keepdims=True)
        diagonal = lax.broadcasted_iota(jnp.int32, (rows, rows), 0) == lax.broadcasted_iota(
            jnp.int32, (rows, rows), 1
        )
        target = jnp.sum(jnp.where(diagonal, wanted[block], 0), axis=1, keepdims=True)
        column = lax.broadcasted_iota(jnp.int32, logits.shape, 1) + v * columns
        picked = jnp.sum(jnp.where(column == target, logits, 0.0), axis=1, keepdims=True)
        maximum, expsum, picked = (
            jnp.sum(jnp.where(diagonal, values, 0.0), axis=0, keepdims=True)
            for values in (maximum, expsum, picked)
        )
        line = lax.broadcasted_iota(jnp.int32, (8, rows), 0)
        return jnp.where(line == 0, maximum, jnp.where(line == 1, expsum, picked))

    def give_stats(block):
        stats[block] = row_stats(block)
        stat_copy(block).start()

    for h in range(2):
        swaps[h].wait_recv()
        for direction in range(2):
            hop(direction, 0, 2 + h).start()
    for copy in own:
        copy.wait()
    head_swap.wait_recv()
    multiply(v)
    part_copy(v).start()

    def step(d):
        for ch in (4, 0, 1, 2, 3):
            for direction in range(2):
                arrived(direction, d, ch)
                hop(direction, d, ch).start()

    def compute(d):
        for direction in range(2):
            block = block_at(direction, d)
            multiply(block)
            part_copy(block).start()

    step(1)
    compute(1)
    gathered[v] = row_stats(v)

    @pl.loop(2, half - 1)
    def _(d):
        step(d)
        compute(d)
        for direction in range(2):
            give_stats(block_at(direction, d - 1))

    last = half - 1
    final = ((4, 2, 0), (3, 1))
    for direction in range(2):
        arrived(direction, last, 4)
    hop(0, last, 4).start()
    for ch in (0, 1):
        for direction in range(2):
            arrived(direction, last, ch)
    for ch in (2, 3):
        for direction in range(2):
            arrived(direction, last, ch)
            if ch in final[direction]:
                hop(direction, last, ch).start()
    hop(0, last, 0).start()
    hop(1, last, 1).start()
    compute(last)
    for direction in range(2):
        give_stats(block_at(direction, last - 1))

    far = block_at(0, half)
    arrived(0, half, 4)
    arrived(0, half, 2)
    arrived(1, half, 3)
    multiply_unit(far, 1 - y)
    part_copy(far).start()
    for direction in range(2):
        give_stats(block_at(direction, last))
    arrived(0, half, 0)
    arrived(1, half, 1)
    multiply_unit(far, y)
    give_stats(far)

    for swap in (*swaps, head_swap):
        swap.wait_send()

    @pl.loop(0, last)
    def _(d):
        for direction in range(2):
            for ch in range(5):
                hop(direction, d, ch).wait_send()

    for direction in range(2):
        for ch in final[direction]:
            hop(direction, last, ch).wait_send()

    @pl.loop(0, n)
    def _(block):
        part_copy(block).wait_send()

    @pl.loop(1, n)
    def _(d):
        stat_copy(block_at(0, d)).wait_send()
        peer = block_at(0, d)
        remote(
            stats.at[peer], gathered.at[peer], stat_tx.at[peer], stat_rx.at[peer], (peer, s)
        ).wait_recv()

    maxima, expsums, picked = (gathered[:, i, :] for i in range(3))
    maximum = jnp.max(maxima, axis=0, keepdims=True)
    expsum = jnp.sum(expsums * jnp.exp(maxima - maximum), axis=0, keepdims=True)
    out[...] = jnp.sum(picked, axis=0, keepdims=True) - (maximum + jnp.log(expsum))


def local(hidden, head_matrix, targets):
    n = lax.axis_size("vocab")
    half = n // 2
    rows = hidden.shape[0]
    width, columns = head_matrix.shape
    dma = pltpu.SemaphoreType.DMA
    result = pl.pallas_call(
        functools.partial(kernel, n),
        out_shape=jax.ShapeDtypeStruct((1, rows), jnp.float32),
        in_specs=[pl.BlockSpec(memory_space=pl.ANY)] * 3,
        out_specs=pl.BlockSpec(memory_space=pltpu.VMEM),
        scratch_shapes=[
            pltpu.VMEM((n, 2, 2, rows, width), jnp.bfloat16),
            pltpu.VMEM((2, width, columns), jnp.bfloat16),
            pltpu.VMEM((n, 1, rows), jnp.int32),
            pltpu.VMEM((n, 2, rows, columns), jnp.float32),
            pltpu.VMEM((n, rows, columns), jnp.float32),
            pltpu.VMEM((n, 8, rows), jnp.float32),
            pltpu.VMEM((n, 8, rows), jnp.float32),
            dma((4,)),
            dma((3,)),
            dma((3,)),
            dma((2, half, 5)),
            dma((2, half + 1, 5)),
            dma((n,)),
            dma((n,)),
            dma((n,)),
            dma((n,)),
        ],
        compiler_params=pltpu.CompilerParams(
            collective_id=0, has_side_effects=True, vmem_limit_bytes=62 * 1024 * 1024
        ),
    )(hidden, head_matrix, targets.reshape(1, rows))
    return result.reshape(rows)


def solution(mesh):
    return jax.shard_map(
        local,
        mesh=mesh,
        in_specs=(P(("vocab", "seq"), None), P("seq", "vocab"), P(("vocab", "seq"))),
        out_specs=P(("vocab", "seq")),
        check_vma=False,
    )
```

time: 246 us -> 73.8 us (0.30)
  waiting for transfers between devices: 191 us -> 0 us
  Pallas kernels: 0 us -> 72.4 us
  between operations: 14.1 us -> 0.01 us
  blocking collectives: 13.1 us -> 0 us
  starting transfers between devices: 12.1 us -> 0 us
  matrix products: 11 us -> 0 us
    all_gather x2 -> x0, waiting for transfers between devices: 172 us -> none  [the longest x1 93.7 us: local(): full_head = lax.all_gather(head_matrix, 'seq', axis=0, tiled=True)]
    pallas_call x0 -> x1, Pallas kernels: none -> 72.4 us  [local(): pl.pallas_call(functools.partial(kernel, n), out_shape=jax.ShapeDtypeStru...]
    all_to_all x3 -> x0, waiting for transfers between devices: 17.4 us -> none  [local(): lax.all_to_all(shaped, 'vocab', split_axis=0, concat_axis=0, tiled=True)]
    unnamed x1 -> x0, blocking collectives: 13.1 us -> none
    all_to_all x3 -> x0, starting transfers between devices: 12.1 us -> none  [local(): lax.all_to_all(shaped, 'vocab', split_axis=0, concat_axis=0, tiled=True)]
    dot_general x1 -> x0, matrix products: 11 us -> none  [local(): jnp.dot(lax.all_gather(hidden, 'vocab', axis=0, tiled=True), full_head, p...]
  transfers between devices with their start and end apart: 5 -> 0, of which waited for: 5 -> 0; matrix products, arithmetic and copies ran while one was open for 1% -> 0% of each run, Pallas kernels for 0% -> 0%
where the time goes in v1:
time: 73.8 us; the launch traced here: 73.6 us
  Pallas kernels  72.4 us (98%)
  local copies, waits for them, and re-layouts  1.19 us (2%)
    pallas_call x1, Pallas kernels, local(): pl.pallas_call(functools.partial(kernel, n), out_shape=jax.ShapeDtypeStru...  72.4 us

profile of v1, /device:TPU:0, one launch (start us, length us, event | category | flops | bytes accessed | tf_op | source)
XLA Modules:
  0.0 73.6 jit_solution(2488982975995222327)
XLA Ops:
  0.0 72.4 %shard_map.37 = f32[1,48]{1,0:T(1,128)} custom-call(bf16[48,7168]{1,0:T(8,128)(2,1)} %hidden.1, bf16[1792,1024]{1,0:T(8,128)(2,1)} %head.1, s32[1,48]{1,0:T(1,128)} %bitcast.2), custom_call_target="tpu_custom_call" | custom-call | tf_op jit(solution)/shard_map/pallas_call | solution.py:247
  72.5 1.2 %copy.5 = f32[48]{0:T(128)} copy(f32[48]{0:T(128)} %bitcast.3) | data formatting | bytes 384

commit v2 on v1

--- a/solution.py
+++ b/solution.py
@@ -22,7 +22,7 @@
 def kernel(
     n, hidden, head, targets, out,
     x, w, wanted, part, other, stats, gathered,
-    local_sem, swap_tx, swap_rx, ring_tx, ring_rx, part_tx, part_rx, stat_tx, stat_rx,
+    local_sem, swap_tx, swap_rx, ring_tx, ring_rx, part_tx, part_rx, far_tx, far_rx, stat_tx, stat_rx,
 ):
     half = n // 2
     width = head.shape[0]
@@ -41,7 +41,6 @@
     barrier = pltpu.get_barrier_semaphore()
     for device in (*ring, y_mate, c_mate):
         pl.semaphore_signal(barrier, inc=1, device_id=device, device_id_type=MESH)
-    pl.semaphore_wait(barrier, 4)
 
     def remote(src, dst, tx, rx, device):
         return pltpu.make_async_remote_copy(
@@ -72,7 +71,15 @@
         start = pl.multiple_of((half_y * 2 + h) * width, width)
         return hidden.at[:, pl.ds(start, width)]
 
-    own = []
+    own = [
+        pltpu.make_async_copy(head, w.at[c], local_sem.at[0]),
+        pltpu.make_async_copy(targets, wanted.at[v], local_sem.at[1]),
+    ]
+    for h in range(2):
+        own.append(pltpu.make_async_copy(hidden_piece(y, h), x.at[v, h, y], local_sem.at[2 + h]))
+    for copy in own:
+        copy.start()
+    pl.semaphore_wait(barrier, 4)
     for h in range(2):
         for direction in range(2):
             hop(direction, 0, h, hidden_piece(y, h)).start()
@@ -85,12 +92,6 @@
         hop(direction, 0, 4, targets).start()
     head_swap = remote(head, w.at[c], swap_tx.at[2], swap_rx.at[2], c_mate)
     head_swap.start()
-    own.append(pltpu.make_async_copy(head, w.at[c], local_sem.at[0]))
-    own.append(pltpu.make_async_copy(targets, wanted.at[v], local_sem.at[1]))
-    for h in range(2):
-        own.append(pltpu.make_async_copy(hidden_piece(y, h), x.at[v, h, y], local_sem.at[2 + h]))
-    for copy in own:
-        copy.start()
 
     def multiply(block):
         @pl.loop(0, columns // tile)
@@ -104,24 +105,38 @@
                 total = term if total is None else total + term
             part[block, :, :, at] = total.reshape(2, rows, tile)
 
-    def multiply_unit(block, unit):
+    def multiply_tile(blocks, unit, j):
+        at = pl.ds(j * tile if isinstance(j, int) else pl.multiple_of(j * tile, tile), tile)
+        total = None
+        for h in range(2):
+            lines = [x[block, h, unit] for block in blocks]
+            term = jnp.dot(
+                lines[0] if len(lines) == 1 else jnp.concatenate(lines, axis=0),
+                w[h, :, at],
+                preferred_element_type=jnp.float32,
+            )
+            total = term if total is None else total + term
+        for i, block in enumerate(blocks):
+            part[block, unit, :, at] = total[i * rows : (i + 1) * rows]
+
+    def multiply_units(blocks, unit):
         @pl.loop(0, columns // tile)
         def _(j):
-            at = pl.ds(pl.multiple_of(j * tile, tile), tile)
-            total = None
-            for h in range(2):
-                term = jnp.dot(x[block, h, unit], w[h, :, at], preferred_element_type=jnp.float32)
-                total = term if total is None else total + term
-            part[block, unit, :, at] = total
+            multiply_tile(blocks, unit, j)
 
     def part_copy(block):
         return remote(part.at[block, 1 - y], other.at[block], part_tx.at[block], part_rx.at[block], y_mate)
 
+    def far_copy(block, j):
+        at = pl.ds(j * tile, tile)
+        return remote(
+            part.at[block, 1 - y, :, at], other.at[block, :, at], far_tx.at[j], far_rx.at[j], y_mate
+        )
+
     def stat_copy(block):
         return remote(stats.at[block], gathered.at[v], stat_tx.at[block], stat_rx.at[v], (block, s))
 
     def row_stats(block):
-        part_copy(block).wait_recv()
         logits = part[block, y] + other[block]
         maximum = jnp.max(logits, axis=1, keepdims=True)
         expsum = jnp.sum(jnp.exp(logits - maximum), axis=1, keepdims=True)
@@ -139,6 +154,7 @@
         return jnp.where(line == 0, maximum, jnp.where(line == 1, expsum, picked))
 
     def give_stats(block):
+        part_copy(block).wait_recv()
         stats[block] = row_stats(block)
         stat_copy(block).start()
 
@@ -152,60 +168,73 @@
     multiply(v)
     part_copy(v).start()
 
-    def step(d):
-        for ch in (4, 0, 1, 2, 3):
+    def pass_on(d, chunks):
+        for ch in chunks:
             for direction in range(2):
                 arrived(direction, d, ch)
                 hop(direction, d, ch).start()
 
-    def compute(d):
-        for direction in range(2):
-            block = block_at(direction, d)
-            multiply(block)
+    def pair(d):
+        return [block_at(direction, d) for direction in range(2)]
+
+    def compute_theirs(d):
+        multiply_units(pair(d), 1 - y)
+        for block in pair(d):
             part_copy(block).start()
 
-    step(1)
-    compute(1)
+    def compute_ours(d):
+        multiply_units(pair(d), y)
+
+    pass_on(1, (4, 0, 2, 1, 3))
+    compute_theirs(1)
+    compute_ours(1)
+    part_copy(v).wait_recv()
     gathered[v] = row_stats(v)
 
     @pl.loop(2, half - 1)
     def _(d):
-        step(d)
-        compute(d)
-        for direction in range(2):
-            give_stats(block_at(direction, d - 1))
+        pass_on(d, (4, 2, 3, 0, 1))
+        compute_theirs(d)
+        compute_ours(d)
+        for block in pair(d - 1):
+            give_stats(block)
 
     last = half - 1
     final = ((4, 2, 0), (3, 1))
-    for direction in range(2):
-        arrived(direction, last, 4)
-    hop(0, last, 4).start()
-    for ch in (0, 1):
-        for direction in range(2):
-            arrived(direction, last, ch)
-    for ch in (2, 3):
-        for direction in range(2):
-            arrived(direction, last, ch)
-            if ch in final[direction]:
-                hop(direction, last, ch).start()
-    hop(0, last, 0).start()
-    hop(1, last, 1).start()
-    compute(last)
-    for direction in range(2):
-        give_stats(block_at(direction, last - 1))
+
+    def pass_half(chunks):
+        for ch in chunks:
+            for direction in range(2):
+                arrived(direction, last, ch)
+                if ch in final[direction]:
+                    hop(direction, last, ch).start()
+
+    pass_half((4, 2, 3))
+    compute_theirs(last)
+    pass_half((0,))
+    for block in pair(last - 1):
+        give_stats(block)
+    pass_half((1,))
+    compute_ours(last)
 
     far = block_at(0, half)
     arrived(0, half, 4)
     arrived(0, half, 2)
     arrived(1, half, 3)
-    multiply_unit(far, 1 - y)
-    part_copy(far).start()
-    for direction in range(2):
-        give_stats(block_at(direction, last))
+    for j in range(columns // tile):
+        multiply_tile([far], 1 - y, j)
+        if j > 0:
+            far_copy(far, j - 1).start()
+    far_copy(far, columns // tile - 1).start()
+    for block in pair(last):
+        give_stats(block)
     arrived(0, half, 0)
     arrived(1, half, 1)
-    multiply_unit(far, y)
-    give_stats(far)
+    multiply_units([far], y)
+    for j in range(columns // tile):
+        far_copy(far, j).wait_recv()
+    stats[far] = row_stats(far)
+    stat_copy(far).start()
 
     for swap in (*swaps, head_swap):
         swap.wait_send()
@@ -220,9 +249,14 @@
         for ch in final[direction]:
             hop(direction, last, ch).wait_send()
 
-    @pl.loop(0, n)
-    def _(block):
-        part_copy(block).wait_send()
+    for j in range(columns // tile):
+        far_copy(far, j).wait_send()
+    part_copy(v).wait_send()
+
+    @pl.loop(1, half)
+    def _(d):
+        for block in pair(d):
+            part_copy(block).wait_send()
 
     @pl.loop(1, n)
     def _(d):
@@ -264,6 +298,8 @@
             dma((2, half + 1, 5)),
             dma((n,)),
             dma((n,)),
+            dma((columns // min(TILE, columns),)),
+            dma((columns // min(TILE, columns),)),
             dma((n,)),
             dma((n,)),
         ],

time: 73.8 us -> 69 us (0.935)
  Pallas kernels: 72.4 us -> 67.7 us
    pallas_call x1, Pallas kernels: 72.4 us -> 67.7 us  [local(): pl.pallas_call(functools.partial(kernel, n), out_shape=jax.ShapeDtypeStru...]
where the time goes in v2:
time: 69 us; the launch traced here: 68.9 us
  Pallas kernels  67.7 us (98%)
  local copies, waits for them, and re-layouts  1.19 us (2%)
    pallas_call x1, Pallas kernels, local(): pl.pallas_call(functools.partial(kernel, n), out_shape=jax.ShapeDtypeStru...  67.7 us

profile of v2, /device:TPU:0, one launch (start us, length us, event | category | flops | bytes accessed | tf_op | source)
XLA Modules:
  0.0 68.9 jit_solution(8149896429284264761)
XLA Ops:
  0.0 67.7 %shard_map.37 = f32[1,48]{1,0:T(1,128)} custom-call(bf16[48,7168]{1,0:T(8,128)(2,1)} %hidden.1, bf16[1792,1024]{1,0:T(8,128)(2,1)} %head.1, s32[1,48]{1,0:T(1,128)} %bitcast.2), custom_call_target="tpu_custom_call" | custom-call | tf_op jit(solution)/shard_map/pallas_call | solution.py:281
  67.7 1.2 %copy.5 = f32[48]{0:T(128)} copy(f32[48]{0:T(128)} %bitcast.3) | data formatting | bytes 384

commit v3 on v2

--- a/solution.py
+++ b/solution.py
@@ -185,39 +185,54 @@
     def compute_ours(d):
         multiply_units(pair(d), y)
 
-    pass_on(1, (4, 0, 2, 1, 3))
+    pass_on(1, (4, 0, 2, 3, 1))
     compute_theirs(1)
     compute_ours(1)
     part_copy(v).wait_recv()
     gathered[v] = row_stats(v)
 
-    @pl.loop(2, half - 1)
+    last = half - 1
+    ahead = last - 1
+
+    @pl.loop(2, ahead)
     def _(d):
-        pass_on(d, (4, 2, 3, 0, 1))
+        pass_on(d, (4, 2, 3))
         compute_theirs(d)
+        pass_on(d, (0, 1))
         compute_ours(d)
         for block in pair(d - 1):
             give_stats(block)
 
-    last = half - 1
+    far = block_at(0, half)
     final = ((4, 2, 0), (3, 1))
-
-    def pass_half(chunks):
-        for ch in chunks:
-            for direction in range(2):
-                arrived(direction, last, ch)
-                if ch in final[direction]:
-                    hop(direction, last, ch).start()
-
-    pass_half((4, 2, 3))
+    pass_on(ahead, (4, 2, 3))
+    compute_theirs(ahead)
+    for direction in range(2):
+        for ch in (0, 1):
+            arrived(direction, ahead, ch)
+    hop(1, ahead, 1).start()
+    for direction in range(2):
+        arrived(direction, last, 4)
+    hop(0, last, 4).start()
+    arrived(0, last, 2)
+    hop(0, last, 2).start()
+    hop(0, ahead, 0).start()
+    hop(0, ahead, 1).start()
+    compute_ours(ahead)
+    arrived(1, last, 2)
+    arrived(1, last, 3)
+    hop(1, last, 3).start()
+    hop(1, ahead, 0).start()
+    arrived(0, last, 3)
     compute_theirs(last)
-    pass_half((0,))
-    for block in pair(last - 1):
+    for block in pair(ahead - 1):
         give_stats(block)
-    pass_half((1,))
-    compute_ours(last)
-
-    far = block_at(0, half)
+    arrived(1, last, 1)
+    hop(1, last, 1).start()
+    for block in pair(ahead):
+        give_stats(block)
+    arrived(0, last, 0)
+    hop(0, last, 0).start()
     arrived(0, half, 4)
     arrived(0, half, 2)
     arrived(1, half, 3)
@@ -226,6 +241,9 @@
         if j > 0:
             far_copy(far, j - 1).start()
     far_copy(far, columns // tile - 1).start()
+    arrived(0, last, 1)
+    arrived(1, last, 0)
+    compute_ours(last)
     for block in pair(last):
         give_stats(block)
     arrived(0, half, 0)

time: 69 us -> 67.5 us (0.978)
  Pallas kernels: 67.7 us -> 66.1 us
    pallas_call x1, Pallas kernels: 67.7 us -> 66.1 us  [local(): pl.pallas_call(functools.partial(kernel, n), out_shape=jax.ShapeDtypeStru...]
where the time goes in v3:
time: 67.5 us; the launch traced here: 67.3 us
  Pallas kernels  66.1 us (98%)
  local copies, waits for them, and re-layouts  1.19 us (2%)
    pallas_call x1, Pallas kernels, local(): pl.pallas_call(functools.partial(kernel, n), out_shape=jax.ShapeDtypeStru...  66.1 us

profile of v3, /device:TPU:0, one launch (start us, length us, event | category | flops | bytes accessed | tf_op | source)
XLA Modules:
  0.0 67.3 jit_solution(1813089120668963838)
XLA Ops:
  0.0 66.1 %shard_map.37 = f32[1,48]{1,0:T(1,128)} custom-call(bf16[48,7168]{1,0:T(8,128)(2,1)} %hidden.1, bf16[1792,1024]{1,0:T(8,128)(2,1)} %head.1, s32[1,48]{1,0:T(1,128)} %bitcast.2), custom_call_target="tpu_custom_call" | custom-call | tf_op jit(solution)/shard_map/pallas_call | solution.py:299
  66.1 1.2 %copy.5 = f32[48]{0:T(128)} copy(f32[48]{0:T(128)} %bitcast.3) | data formatting | bytes 384

commit v4 on v3

--- a/solution.py
+++ b/solution.py
@@ -71,18 +71,18 @@
         start = pl.multiple_of((half_y * 2 + h) * width, width)
         return hidden.at[:, pl.ds(start, width)]
 
+    pieces = [pltpu.make_async_copy(hidden_piece(y, h), x.at[v, h, y], local_sem.at[2 + h]) for h in range(2)]
     own = [
         pltpu.make_async_copy(head, w.at[c], local_sem.at[0]),
         pltpu.make_async_copy(targets, wanted.at[v], local_sem.at[1]),
     ]
-    for h in range(2):
-        own.append(pltpu.make_async_copy(hidden_piece(y, h), x.at[v, h, y], local_sem.at[2 + h]))
-    for copy in own:
+    for copy in (*pieces, *own):
         copy.start()
     pl.semaphore_wait(barrier, 4)
     for h in range(2):
+        pieces[h].wait()
         for direction in range(2):
-            hop(direction, 0, h, hidden_piece(y, h)).start()
+            hop(direction, 0, h).start()
     swaps = [
         remote(hidden_piece(1 - y, h), x.at[v, h, y], swap_tx.at[h], swap_rx.at[h], y_mate) for h in range(2)
     ]

time: 67.5 us -> 67.2 us (level)
  no operation moved by 1% of the time
where the time goes in v4:
time: 67.2 us; the launch traced here: 67.1 us
  Pallas kernels  65.9 us (98%)
  local copies, waits for them, and re-layouts  1.19 us (2%)
    pallas_call x1, Pallas kernels, local(): pl.pallas_call(functools.partial(kernel, n), out_shape=jax.ShapeDtypeStru...  65.9 us

profile of v4, /device:TPU:0, one launch (start us, length us, event | category | flops | bytes accessed | tf_op | source)
XLA Modules:
  0.0 67.1 jit_solution(7272997873006729347)
XLA Ops:
  0.0 65.9 %shard_map.37 = f32[1,48]{1,0:T(1,128)} custom-call(bf16[48,7168]{1,0:T(8,128)(2,1)} %hidden.1, bf16[1792,1024]{1,0:T(8,128)(2,1)} %head.1, s32[1,48]{1,0:T(1,128)} %bitcast.2), custom_call_target="tpu_custom_call" | custom-call | tf_op jit(solution)/shard_map/pallas_call | solution.py:299
  65.9 1.2 %copy.5 = f32[48]{0:T(128)} copy(f32[48]{0:T(128)} %bitcast.3) | data formatting | bytes 384
